TPU v7x, 8 devices: a whole 2x2x1 slice. The times are simulated.
8 devices in a mesh: dp: 1 (over z), row: 2 (over y), col: 4 (over x, core).
Axes of the slice: x: 2, y: 2, z: 1, core: 2. Of those that a mesh axis runs over, the one named last changes fastest.
Arguments:
- x: bfloat16 [1024, 1280], P(('dp', 'row', 'col'))
- route_idx: int32 [1024, 6], P(('dp', 'row', 'col'))
- gates: float32 [1024, 6], P(('dp', 'row', 'col'))
- w1: bfloat16 [160, 1280, 384], P(('row', 'col'))
- w3: bfloat16 [160, 1280, 384], P(('row', 'col'))
- w2: bfloat16 [160, 384, 1280], P(('row', 'col'))
- dy: bfloat16 [1024, 1280], P(('dp', 'row', 'col'))
Outputs:
- output 1: bfloat16 [1024, 1280], P(('dp', 'row', 'col'))
- output 2: bfloat16 [1024, 1280], P(('dp', 'row', 'col'))
- output 3: float32 [1024, 6], P(('dp', 'row', 'col'))
- output 4: float32 [160, 1280, 384], P(('dp', 'row', 'col'))
- output 5: float32 [160, 1280, 384], P(('dp', 'row', 'col'))
- output 6: float32 [160, 384, 1280], P(('dp', 'row', 'col'))
All inputs are finite; a program needn't handle non-finite values.
Results may differ from a plain program's by a relative error of at most 0.0078903.
Values are sent between devices in bfloat16 or wider.
A program may use at most 1 GiB of HBM per device.

v0:
```python
import jax
import jax.numpy as jnp
from jax import lax
from jax.sharding import PartitionSpec as P


def slot_positions(ridx, ne, cap):
    tok, top = ridx.shape
    n = tok * top
    ef = ridx.reshape(n)
    order = jnp.argsort(ef, stable=True).astype(jnp.int32)
    es = ef[order]
    first = jnp.searchsorted(es, es, side='left').astype(jnp.int32)
    rank = jnp.arange(n, dtype=jnp.int32) - first
    pos = jnp.zeros((n,), jnp.int32).at[order].set(es * cap + rank)
    inv = jnp.full((ne * cap,), n, jnp.int32).at[pos].set(jnp.arange(n, dtype=jnp.int32))
    return pos, inv


def to_experts(buf, nd, el, cap):
    d = buf.shape[-1]
    return buf.reshape(nd, el, cap, d).transpose(1, 0, 2, 3).reshape(el, nd * cap, d)


def from_experts(buf, nd, el, cap):
    d = buf.shape[-1]
    return buf.reshape(el, nd, cap, d).transpose(1, 0, 2, 3).reshape(nd, el * cap, d)


def expert_forward(xe, w1, w3, w2):
    u = jnp.einsum('ecd,edf->ecf', xe, w1, preferred_element_type=jnp.float32).astype(jnp.bfloat16)
    v = jnp.einsum('ecd,edf->ecf', xe, w3, preferred_element_type=jnp.float32).astype(jnp.bfloat16)
    uf = u.astype(jnp.float32)
    a = (uf * jax.nn.sigmoid(uf) * v.astype(jnp.float32)).astype(jnp.bfloat16)
    o = jnp.einsum('ecf,efd->ecd', a, w2, preferred_element_type=jnp.float32).astype(jnp.bfloat16)
    return u, v, a, o


def expert_backward(xe, u, v, a, doe, w1, w3, w2):
    gw2 = jnp.einsum('ecf,ecd->efd', a, doe, preferred_element_type=jnp.float32)
    da = jnp.einsum('ecd,efd->ecf', doe, w2, preferred_element_type=jnp.float32)
    uf = u.astype(jnp.float32)
    vf = v.astype(jnp.float32)
    sg = jax.nn.sigmoid(uf)
    du = (da * vf * sg * (1.0 + uf * (1.0 - sg))).astype(jnp.bfloat16)
    dv = (da * uf * sg).astype(jnp.bfloat16)
    gw1 = jnp.einsum('ecd,ecf->edf', xe, du, preferred_element_type=jnp.float32)
    gw3 = jnp.einsum('ecd,ecf->edf', xe, dv, preferred_element_type=jnp.float32)
    dxe = (jnp.einsum('ecf,edf->ecd', du, w1, preferred_element_type=jnp.float32) + jnp.einsum('ecf,edf->ecd', dv, w3, preferred_element_type=jnp.float32)).astype(jnp.bfloat16)
    return gw1, gw3, gw2, dxe


def solution(mesh):
    nd = mesh.shape['row'] * mesh.shape['col']
    grp = ('row', 'col')
    tspec = P(('dp', 'row', 'col'), None)
    wspec = P(grp, None, None)
    gspec = P(('dp', 'row', 'col'), None, None)

    def exchange(buf):
        return lax.all_to_all(buf, grp, 0, 0, tiled=True)

    def local(x, ridx, gates, w1, w3, w2, dy):
        tok, d = x.shape
        top = ridx.shape[1]
        el = w1.shape[0]
        ne = el * nd
        cap = (4 * tok * top + ne - 1) // ne
        n = tok * top
        pos, inv = slot_positions(ridx, ne, cap)
        zrow = jnp.zeros((1, d), x.dtype)
        send = jnp.concatenate([x, zrow])[inv // top].reshape(nd, el * cap, d)
        xe = to_experts(exchange(send), nd, el, cap)
        u, v, a, oe = expert_forward(xe, w1, w3, w2)
        ret = exchange(from_experts(oe, nd, el, cap)).reshape(ne * cap, d)
        ob = ret[pos].reshape(tok, top, d)
        y = jnp.sum(gates[:, :, None] * ob.astype(jnp.float32), axis=1).astype(jnp.bfloat16)
        dgates = jnp.einsum('td,tjd->tj', dy, ob, preferred_element_type=jnp.float32)
        do = (gates[:, :, None] * dy[:, None, :].astype(jnp.float32)).astype(jnp.bfloat16).reshape(n, d)
        dsend = jnp.concatenate([do, zrow])[inv].reshape(nd, el * cap, d)
        doe = to_experts(exchange(dsend), nd, el, cap)
        gw1, gw3, gw2, dxe = expert_backward(xe, u, v, a, doe, w1, w3, w2)
        dret = exchange(from_experts(dxe, nd, el, cap)).reshape(ne * cap, d)
        dx = jnp.sum(dret[pos].reshape(tok, top, d).astype(jnp.float32), axis=1).astype(jnp.bfloat16)
        return y, dx, dgates, gw1, gw3, gw2

    return jax.shard_map(local, mesh=mesh, in_specs=(tspec, tspec, tspec, wspec, wspec, wspec, tspec), out_specs=(tspec, tspec, tspec, gspec, gspec, gspec), check_vma=False)
```

profile of v0, /device:TPU:0, one launch (start us, length us, event | category | flops | bytes accessed | tf_op | source)
XLA Modules:
  0.0 576.0 jit_solution(300599597803696175)
XLA Ops:
  2.5 4.4 sort.17
  10.1 32.8 %while.25 = (s32[]{:T(128)}, u32[768]{0:T(1024)S(1)}, u32[768]{0:T(1024)S(1)}, s32[768]{0:T(1024)S(1)}, s32[]{:T(128)}, /*index=5*/s32[]{:T(128)}, s32[]{}) while((s32[]{:T(128)}, u32[768]{0:T(1024)S(1)}, u32[768]{0:T(1024)S(1)}, s32[768]{0:T(1024)S(1)}, s32[]{:T(128)}, /*index=5*/s32[]{:T(128)}, s32[]{}) %tuple.43), condition=%wide.region_2.3_spmd.clone, body=%wide.region_1.2_spmd.clone.sunk | while | flops 14852 | bytes 57957 | solution.py:13
  10.2 3.2 gather_fusion
  13.5 3.2 gather_fusion
  16.7 3.2 gather_fusion
  20.0 3.2 gather_fusion
  23.3 3.2 gather_fusion
  26.6 3.2 gather_fusion
  29.9 3.2 gather_fusion
  33.2 3.2 gather_fusion
  36.4 3.2 gather_fusion
  39.7 3.2 gather_fusion
  43.0 3.4 scatter_custom_fusion
  46.4 3.4 scatter_custom_fusion.1
  52.5 5.0 mul.65
  60.1 11.4 %gather_fusion.4 = bf16[3200,1280]{1,0:T(8,128)(2,1)} fusion(bf16[769,1280]{1,0:T(8,128)(2,1)S(1)} %concatenate.7, s32[4096]{0:T(1024)S(1)} %get-tuple-element.105), kind=kCustom, calls=%fused_computation.4 | custom fusion | bytes 16396800 | tf_op jit(solution)/shard_map/gather | solution.py:80
  71.5 4.3 all-to-all-start.2
  75.8 11.4 %gather_fusion.2 = bf16[3200,1280]{1,0:T(8,128)(2,1)} fusion(bf16[129,1280]{1,0:T(8,128)(2,1)S(1)} %concatenate.6, s32[4096]{0:T(1024)S(1)} %get-tuple-element.106), kind=kCustom, calls=%fused_computation.2 | custom fusion | bytes 16396800 | tf_op jit(solution)/shard_map/gather | solution.py:72
  87.3 81.0 %all-to-all-done.2 = bf16[8,400,1280]{2,1,0:T(8,128)(2,1)} async-done(((bf16[8,400,1280]{2,1,0:T(8,128)(2,1)}), bf16[8,400,1280]{2,1,0:T(8,128)(2,1)}, u32[]{:S(2)}, u32[]{:S(2)}) %all-to-all-start.2) | async-done | bytes 8192032 | tf_op jit(solution)/shard_map/all_to_all | solution.py:61
  168.3 4.1 all-to-all-start
  173.0 9.4 %copy.32 = bf16[8,400,1280]{2,0,1:T(8,128)(2,1)} copy(bf16[8,400,1280]{2,1,0:T(8,128)(2,1)} %all-to-all-done.2) | data formatting | bytes 16384000 | tf_op jit(solution)/shard_map/all_to_all | solution.py:61
  182.4 9.6 %copy.33 = bf16[20,8,20,1280]{3,2,1,0:T(8,128)(2,1)} copy(bf16[20,8,20,1280]{3,1,2,0:T(8,128)(2,1)} %bitcast.37) | data formatting | bytes 16384000 | tf_op jit(solution)/shard_map/transpose | solution.py:22
  191.9 12.7 %reshape.73 = bf16[20,160,1280]{2,1,0:T(8,128)(2,1)} reshape(bf16[20,8,20,1280]{3,2,1,0:T(8,128)(2,1)} %copy.33) | data formatting | bytes 16384000 | tf_op jit(solution)/shard_map/reshape | solution.py:22
  204.7 59.6 %all-to-all-done = bf16[8,400,1280]{2,1,0:T(8,128)(2,1)} async-done(((bf16[8,400,1280]{2,1,0:T(8,128)(2,1)}), bf16[8,400,1280]{2,1,0:T(8,128)(2,1)}, u32[]{:S(2)}, u32[]{:S(2)}) %all-to-all-start) | async-done | bytes 8192032 | tf_op jit(solution)/shard_map/all_to_all | solution.py:61
  264.3 9.4 %copy.27 = bf16[8,400,1280]{2,0,1:T(8,128)(2,1)} copy(bf16[8,400,1280]{2,1,0:T(8,128)(2,1)} %all-to-all-done) | data formatting | bytes 16384000 | tf_op jit(solution)/shard_map/all_to_all | solution.py:61
  273.7 9.6 %copy.28 = bf16[20,8,20,1280]{3,2,1,0:T(8,128)(2,1)} copy(bf16[20,8,20,1280]{3,1,2,0:T(8,128)(2,1)} %bitcast.38) | data formatting | bytes 16384000 | tf_op jit(solution)/shard_map/transpose | solution.py:22
  283.2 12.8 %reshape.66 = bf16[20,160,1280]{2,1,0:T(8,128)(2,1)} reshape(bf16[20,8,20,1280]{3,2,1,0:T(8,128)(2,1)} %copy.28) | data formatting | bytes 16384000 | tf_op jit(solution)/shard_map/reshape | solution.py:22
  296.0 13.4 %convolution_convert_fusion.2 = bf16[20,160,384]{2,1,0:T(8,128)(2,1)S(1)} fusion(bf16[20,160,1280]{2,1,0:T(8,128)(2,1)} %reshape.66, bf16[20,1280,384]{2,1,0:T(8,128)(2,1)} %param.12), kind=kOutput, calls=%fused_computation.34 | convolution fusion | flops 3146956800 | bytes 30310400 | tf_op jit(solution)/shard_map/ecd,edf->ecf/dot_general | solution.py:31
  309.4 14.8 %convolution_convert_fusion.1 = bf16[20,160,384]{2,1,0:T(8,128)(2,1)} fusion(bf16[20,160,1280]{2,1,0:T(8,128)(2,1)} %reshape.66, bf16[20,1280,384]{2,1,0:T(8,128)(2,1)} %param.13), kind=kOutput, calls=%fused_computation.33 | convolution fusion | flops 3146956800 | bytes 30310400 | tf_op jit(solution)/shard_map/ecd,edf->ecf/dot_general | solution.py:32
  324.2 15.6 %convolution_convert_fusion = bf16[20,160,1280]{2,1,0:T(8,128)(2,1)} fusion(bf16[20,384,1280]{2,1,0:T(8,128)(2,1)} %param.14, bf16[20,160,384]{2,1,0:T(8,128)(2,1)} %convolution_convert_fusion.1, bf16[20,160,384]{2,1,0:T(8,128)(2,1)S(1)} %convolution_convert_fusion.2), kind=kOutput, calls=%fused_computation.14 | convolution fusion | flops 3159654400 | bytes 32768000 | tf_op jit(solution)/shard_map/ecf,efd->ecd/dot_general | solution.py:35
  339.8 12.5 %reshape.67 = bf16[20,8,20,1280]{3,2,1,0:T(8,128)(2,1)} reshape(bf16[20,160,1280]{2,1,0:T(8,128)(2,1)} %convolution_convert_fusion) | data formatting | bytes 16384000 | tf_op jit(solution)/shard_map/reshape | solution.py:27
  352.3 9.2 %copy.29 = bf16[8,20,20,1280]{3,0,2,1:T(8,128)(2,1)} copy(bf16[8,20,20,1280]{3,2,0,1:T(8,128)(2,1)} %bitcast.33) | data formatting | bytes 16384000 | tf_op jit(solution)/shard_map/transpose | solution.py:27
  361.5 8.3 %copy.30 = bf16[8,400,1280]{2,1,0:T(8,128)(2,1)} copy(bf16[8,400,1280]{2,0,1:T(8,128)(2,1)} %bitcast.39) | data formatting | bytes 16384000 | tf_op jit(solution)/shard_map/reshape | solution.py:27
  369.8 3.7 all-to-all-start.1
  373.5 15.0 %fusion.4 = (bf16[20,160,384]{2,1,0:T(8,128)(2,1)}, f32[20,160,384]{2,1,0:T(8,128)}) fusion(bf16[20,160,384]{2,1,0:T(8,128)(2,1)} %convolution_convert_fusion.1, bf16[20,160,384]{2,1,0:T(8,128)(2,1)S(1)} %convolution_convert_fusion.2, bf16[20,160,1280]{2,1,0:T(8,128)(2,1)} %reshape.73, bf16[20,384,1280]{2,1,0:T(8,128)(2,1)} %param.14), kind=kOutput, calls=%fused_computation.25 | convolution fusion | flops 3160473600 | bytes 40140800 | tf_op jit(solution)/shard_map/ecd,efd->ecf/dot_general | solution.py:41
  388.5 15.4 %fusion.24 = f32[20,160,1280]{2,1,0:T(8,128)} fusion(bf16[20,160,384]{2,1,0:T(8,128)(2,1)} %get-tuple-element.103, bf16[20,1280,384]{2,1,0:T(8,128)(2,1)} %param.12), kind=kOutput, calls=%fused_computation.56 | convolution fusion | flops 3145728000 | bytes 38502400 | tf_op jit(solution)/shard_map/ecf,edf->ecd/dot_general | solution.py:49
  403.9 18.0 %fusion = bf16[20,160,1280]{2,1,0:T(8,128)(2,1)} fusion(f32[20,160,1280]{2,1,0:T(8,128)} %fusion.24, bf16[20,1280,384]{2,1,0:T(8,128)(2,1)} %param.13, f32[20,160,384]{2,1,0:T(8,128)} %get-tuple-element.104, bf16[20,160,384]{2,1,0:T(8,128)(2,1)S(1)} %convolution_convert_fusion.2), kind=kOutput, calls=%fused_computation.13 | convolution fusion | flops 3162521600 | bytes 51609600 | tf_op jit(solution)/shard_map/ecf,edf->ecd/dot_general | solution.py:49
  421.9 12.5 %reshape.74 = bf16[20,8,20,1280]{3,2,1,0:T(8,128)(2,1)} reshape(bf16[20,160,1280]{2,1,0:T(8,128)(2,1)} %fusion) | data formatting | bytes 16384000 | tf_op jit(solution)/shard_map/reshape | solution.py:27
  434.5 9.2 %copy.34 = bf16[8,20,20,1280]{3,0,2,1:T(8,128)(2,1)} copy(bf16[8,20,20,1280]{3,2,0,1:T(8,128)(2,1)} %bitcast.34) | data formatting | bytes 16384000 | tf_op jit(solution)/shard_map/transpose | solution.py:27
  443.7 8.1 %copy.35 = bf16[8,400,1280]{2,1,0:T(8,128)(2,1)} copy(bf16[8,400,1280]{2,0,1:T(8,128)(2,1)} %bitcast.40) | data formatting | bytes 16384000 | tf_op jit(solution)/shard_map/reshape | solution.py:27
  451.8 13.6 %all-to-all-done.1 = bf16[8,400,1280]{2,1,0:T(8,128)(2,1)} async-done(((bf16[8,400,1280]{2,1,0:T(8,128)(2,1)}), bf16[8,400,1280]{2,1,0:T(8,128)(2,1)}, u32[]{:S(2)}, u32[]{:S(2)}) %all-to-all-start.1) | async-done | bytes 8192032 | tf_op jit(solution)/shard_map/all_to_all | solution.py:61
  465.3 3.9 all-to-all-start.3
  469.2 20.2 %fusion.25 = f32[20,1280,384]{2,1,0:T(8,128)} fusion(bf16[20,160,1280]{2,1,0:T(8,128)(2,1)} %reshape.66, bf16[20,160,384]{2,1,0:T(8,128)(2,1)} %get-tuple-element.103), kind=kOutput, calls=%fused_computation.57 | convolution fusion | flops 3145728000 | bytes 49971200 | tf_op jit(solution)/shard_map/ecd,ecf->edf/dot_general | solution.py:47
  489.5 23.0 %fusion.18 = f32[20,384,1280]{2,1,0:T(8,128)} fusion(bf16[20,160,1280]{2,1,0:T(8,128)(2,1)} %reshape.73, bf16[20,160,384]{2,1,0:T(8,128)(2,1)} %convolution_convert_fusion.1, bf16[20,160,384]{2,1,0:T(8,128)(2,1)S(1)} %convolution_convert_fusion.2), kind=kOutput, calls=%fused_computation.54 | convolution fusion | flops 3155558400 | bytes 52428800 | tf_op jit(solution)/shard_map/ecf,ecd->efd/dot_general | solution.py:40
  512.5 20.4 %fusion.21 = f32[20,1280,384]{2,1,0:T(8,128)} fusion(bf16[20,160,1280]{2,1,0:T(8,128)(2,1)} %reshape.66, f32[20,160,384]{2,1,0:T(8,128)} %get-tuple-element.104, bf16[20,160,384]{2,1,0:T(8,128)(2,1)S(1)} %convolution_convert_fusion.2), kind=kOutput, calls=%fused_computation.55 | convolution fusion | flops 3154329600 | bytes 54886400 | tf_op jit(solution)/shard_map/ecd,ecf->edf/dot_general | solution.py:48
  532.9 9.6 %gather_fusion.3 = bf16[768,1280]{1,0:T(8,128)(2,1)} fusion(bf16[3200,1280]{1,0:T(8,128)(2,1)} %bitcast.5, s32[1024]{0:T(1024)S(1)} %copy-done.5), kind=kCustom, calls=%fused_computation.3 | custom fusion | bytes 3935232 | tf_op jit(solution)/shard_map/gather | solution.py:76
  550.0 11.1 %all-to-all-done.3 = bf16[8,400,1280]{2,1,0:T(8,128)(2,1)} async-done(((bf16[8,400,1280]{2,1,0:T(8,128)(2,1)}), bf16[8,400,1280]{2,1,0:T(8,128)(2,1)}, u32[]{:S(2)}, u32[]{:S(2)}) %all-to-all-start.3) | async-done | bytes 8192032 | tf_op jit(solution)/shard_map/all_to_all | solution.py:61
  561.1 9.6 %gather_fusion.5 = bf16[768,1280]{1,0:T(8,128)(2,1)} fusion(bf16[3200,1280]{1,0:T(8,128)(2,1)} %bitcast.11, s32[1024]{0:T(1024)S(1)} %copy-done.5), kind=kCustom, calls=%fused_computation.5 | custom fusion | bytes 3935232 | tf_op jit(solution)/shard_map/gather | solution.py:84
  (88 shorter events, 23.9 us)
Async XLA Ops:
  1.4 8.7 %copy-start = (f32[128,6]{1,0:T(8,128)}, f32[128,6]{1,0:T(8,128)S(1)}, u32[]{:S(2)}) copy-start(f32[128,6]{1,0:T(8,128)S(1)} %copy.25) | copy-start | bytes 9220
  10.1 39.7 %copy-start.3 = (bf16[128,1280]{1,0:T(8,128)(2,1)S(1)}, bf16[128,1280]{1,0:T(8,128)(2,1)}, u32[]{:S(2)}) copy-start(bf16[128,1280]{1,0:T(8,128)(2,1)} %param.15) | copy-start | bytes 983044
  71.5 4.3 copy-start.2
  71.5 96.8 %all-to-all-start.2 = ((bf16[8,400,1280]{2,1,0:T(8,128)(2,1)}), bf16[8,400,1280]{2,1,0:T(8,128)(2,1)}, u32[]{:S(2)}, u32[]{:S(2)}) async-start(bf16[8,400,1280]{2,1,0:T(8,128)(2,1)} %bitcast.36), calls=%async_computation.2 | async-start | bytes 16384000 | tf_op jit(solution)/shard_map/all_to_all | solution.py:61
  168.3 96.0 %all-to-all-start = ((bf16[8,400,1280]{2,1,0:T(8,128)(2,1)}), bf16[8,400,1280]{2,1,0:T(8,128)(2,1)}, u32[]{:S(2)}, u32[]{:S(2)}) async-start(bf16[8,400,1280]{2,1,0:T(8,128)(2,1)} %bitcast.35), calls=%async_computation | async-start | bytes 16384000 | tf_op jit(solution)/shard_map/all_to_all | solution.py:61
  369.8 95.6 %all-to-all-start.1 = ((bf16[8,400,1280]{2,1,0:T(8,128)(2,1)}), bf16[8,400,1280]{2,1,0:T(8,128)(2,1)}, u32[]{:S(2)}, u32[]{:S(2)}) async-start(bf16[8,400,1280]{2,1,0:T(8,128)(2,1)} %copy.30), calls=%async_computation.1 | async-start | bytes 16384000 | tf_op jit(solution)/shard_map/all_to_all | solution.py:61
  465.3 95.8 %all-to-all-start.3 = ((bf16[8,400,1280]{2,1,0:T(8,128)(2,1)}), bf16[8,400,1280]{2,1,0:T(8,128)(2,1)}, u32[]{:S(2)}, u32[]{:S(2)}) async-start(bf16[8,400,1280]{2,1,0:T(8,128)(2,1)} %copy.35), calls=%async_computation.3 | async-start | bytes 16384000 | tf_op jit(solution)/shard_map/all_to_all | solution.py:61
  512.5 20.4 %copy-start.5 = (s32[1024]{0:T(1024)S(1)}, s32[1024]{0:T(1024)}, u32[]{:S(2)}) copy-start(s32[1024]{0:T(1024)} %pad_clamp_fusion.3) | copy-start | bytes 12292
  532.9 12.3 %copy-start.4 = (bf16[128,1280]{1,0:T(8,128)(2,1)S(1)}, bf16[128,1280]{1,0:T(8,128)(2,1)}, u32[]{:S(2)}) copy-start(bf16[128,1280]{1,0:T(8,128)(2,1)} %param.15) | copy-start | bytes 983044
  542.5 4.9 copy-start.1
where the time goes:
time: 583 us; the launch traced here: 576 us
  local copies, waits for them, and re-layouts  223 us (38%)
  waiting for transfers between devices  165 us (28%)
  matrix products  157 us (27%)
  starting transfers between devices  16 us (3%)
  other arithmetic  12.9 us (2%)
    all_to_all x4, waiting for transfers between devices, exchange(): return lax.all_to_all(buf, grp, 0, 0, tiled=True)  165 us
    reshape x4, local copies, waits for them, and re-layouts, from_experts(): buf.reshape(el, nd, cap, d).transpose(1, 0, 2, 3).reshape(nd, el * cap, d)  41.4 us
    gather x10, local copies, waits for them, and re-layouts, slot_positions(): first = jnp.searchsorted(es, es, side='left').astype(jnp.int32)  31.9 us
    reshape x2, local copies, waits for them, and re-layouts, to_experts(): buf.reshape(nd, el, cap, d).transpose(1, 0, 2, 3).reshape(el, nd * cap, d)  25.5 us
    dot_general x1, matrix products, expert_backward(): gw2 = jnp.einsum('ecf,ecd->efd', a, doe, preferred_element_type=jnp.float32)  23 us
    dot_general x1, matrix products, expert_backward(): gw3 = jnp.einsum('ecd,ecf->edf', xe, dv, preferred_element_type=jnp.float32)  20.4 us
    dot_general x1, matrix products, expert_backward(): gw1 = jnp.einsum('ecd,ecf->edf', xe, du, preferred_element_type=jnp.float32)  20.2 us
    transpose x2, local copies, waits for them, and re-layouts, to_experts(): buf.reshape(nd, el, cap, d).transpose(1, 0, 2, 3).reshape(el, nd * cap, d)  19.1 us
  transfers between devices with their start and end apart: 4, of which 4 were waited for; matrix products, arithmetic and copies ran while one was open for 35% of the time, Pallas kernels for 0%

commit v1 on v0

v1 whole, which is shorter than its diff:
```python
import functools

import jax
import jax.numpy as jnp
from jax import lax
from jax.experimental import pallas as pl
from jax.experimental.pallas import tpu as pltpu
from jax.sharding import PartitionSpec as P

ND = 8
CAP = 24
BF = jnp.bfloat16
F32 = jnp.float32
VMEM_LIMIT = 60 * 1024 * 1024


def dot(a, b):
    return jnp.dot(a, b, preferred_element_type=F32)


def dot_nt(a, b):
    return lax.dot_general(a, b, (((1,), (1,)), ((), ())), preferred_element_type=F32)


def dot_tn(a, b):
    return lax.dot_general(a, b, (((0,), (0,)), ((), ())), preferred_element_type=F32)


def params(n=1):
    return pltpu.CompilerParams(dimension_semantics=("arbitrary",) * n, vmem_limit_bytes=VMEM_LIMIT)


def cost(flops, nbytes):
    return pl.CostEstimate(flops=int(flops), bytes_accessed=int(nbytes), transcendentals=0)


def whole(shape):
    return pl.BlockSpec(shape, lambda *_: (0,) * len(shape))


def select_rows(rank, el):
    r = lax.broadcasted_iota(jnp.int32, (CAP, rank.shape[1]), 0).astype(F32)
    return jnp.concatenate([jnp.where(rank[e:e + 1, :] == r, 1.0, 0.0) for e in range(el)], axis=0)


def expand_rows(mat, el):
    return jnp.concatenate([jnp.broadcast_to(mat[e:e + 1, :], (CAP, mat.shape[1])) for e in range(el)], axis=0)


def split3(g):
    hi = g.astype(BF)
    rest = g - hi.astype(F32)
    mid = rest.astype(BF)
    low = (rest - mid.astype(F32)).astype(BF)
    return hi, mid, low


def route_kernel(p_ref, meta_ref, rank_ref, gate_ref, *, el, top):
    p = p_ref[0]
    tok = meta_ref.shape[2]
    ep = rank_ref.shape[1]
    eid = (lax.broadcasted_iota(jnp.int32, (ep, tok), 0) + p * el).astype(F32)
    live = lax.broadcasted_iota(jnp.int32, (ep, tok), 0) < el
    before = (lax.broadcasted_iota(jnp.int32, (tok, tok), 0) < lax.broadcasted_iota(jnp.int32, (tok, tok), 1))
    before = jnp.where(before, 1.0, 0.0).astype(BF)
    for s in range(ND):
        m = meta_ref[p ^ s]
        hit = jnp.zeros((ep, tok), F32)
        gate = jnp.zeros((ep, tok), F32)
        for j in range(top):
            same = (m[j:j + 1, :] == eid) & live
            hit = hit + jnp.where(same, 1.0, 0.0)
            gate = gate + jnp.where(same, m[8 + j:9 + j, :], 0.0)
        rank = dot(hit.astype(BF), before)
        rank_ref[s] = jnp.where(hit > 0.0, rank, -1.0)
        gate_ref[s] = gate


def gather_experts(rank_ref, srcs, out_ref, el, gate_ref=None):
    d = srcs[0].shape[1]
    step = 256
    for q in range(ND // 2):
        sel = [select_rows(rank_ref[2 * q + h], el) for h in range(2)]
        if gate_ref is not None:
            g = [jnp.sum(sel[h] * expand_rows(gate_ref[2 * q + h], el), axis=1, keepdims=True) for h in range(2)]
        sel = [m.astype(BF) for m in sel]
        for n in range(0, d, step):
            rows = [dot(sel[h], srcs[2 * q + h][:, n:n + step]) for h in range(2)]
            if gate_ref is not None:
                rows = [rows[h] * g[h] for h in range(2)]
            for e in range(el):
                part = jnp.concatenate([rows[h][e * CAP:(e + 1) * CAP] for h in range(2)], axis=0)
                out_ref[e, 2 * q * CAP:(2 * q + 2) * CAP, n:n + step] = part.astype(BF)


def up_kernel(rank_ref, *refs, el):
    srcs = refs[:ND]
    w1_ref, w3_ref, u_ref, v_ref, a_ref, xs_ref = refs[ND:]
    e = pl.program_id(0)

    @pl.when(e == 0)
    def _():
        gather_experts(rank_ref, srcs, xs_ref, el)

    xs = xs_ref[e]
    u = dot(xs, w1_ref[0]).astype(BF)
    v = dot(xs, w3_ref[0]).astype(BF)
    uf = u.astype(F32)
    u_ref[0] = u
    v_ref[0] = v
    a_ref[0] = (uf * jax.nn.sigmoid(uf) * v.astype(F32)).astype(BF)


def to_sources(rows, out_ref):
    for s in range(ND):
        part = jnp.concatenate([r[s * CAP:(s + 1) * CAP] for r in rows], axis=0)
        out_ref[s] = part.astype(BF)


def down_kernel(a_ref, w2_ref, o_ref):
    to_sources([dot(a_ref[h], w2_ref[h]) for h in range(2)], o_ref)


def combine_y_kernel(p_ref, rank_ref, gate_ref, o_ref, dy_ref, send_ref, keep_ref, dg_ref, *, el):
    i = pl.program_id(0)
    sel = select_rows(rank_ref[0], el)
    gexp = expand_rows(gate_ref[0], el)
    o = o_ref[0]
    y = None
    for piece in split3(sel * gexp):
        part = dot_tn(piece, o)
        y = part if y is None else y + part

    @pl.when(i < ND // 2)
    def _():
        send_ref[0] = y

    @pl.when(i >= ND // 2)
    def _():
        keep_ref[0] = y

    dys = dot(sel.astype(BF), dy_ref[0])
    dg = jnp.sum(dys * o.astype(F32), axis=1, keepdims=True)
    spread = sel * dg
    rows = [jnp.sum(spread[e * CAP:(e + 1) * CAP], axis=0, keepdims=True) for e in range(el)]
    rows.append(jnp.zeros((dg_ref.shape[1] - el, sel.shape[1]), F32))
    dg_ref[0] = jnp.concatenate(rows, axis=0)


def combine_dx_kernel(rank_ref, o_ref, send_ref, keep_ref, *, el):
    i = pl.program_id(0)
    dx = dot_tn(select_rows(rank_ref[0], el).astype(BF), o_ref[0])

    @pl.when(i < ND // 2)
    def _():
        send_ref[0] = dx

    @pl.when(i >= ND // 2)
    def _():
        keep_ref[0] = dx


def act_kernel(rank_ref, gate_ref, *refs, el):
    srcs = refs[:ND]
    w2_ref, u_ref, v_ref, a_ref, du_ref, dv_ref, gw2_ref, do_ref = refs[ND:]
    e = pl.program_id(0)

    @pl.when(e == 0)
    def _():
        gather_experts(rank_ref, srcs, do_ref, el, gate_ref)

    do = do_ref[e]
    gw2_ref[0] = dot_tn(a_ref[0], do)
    da = dot_nt(do, w2_ref[0])
    u = u_ref[0].astype(F32)
    v = v_ref[0].astype(F32)
    sg = jax.nn.sigmoid(u)
    du_ref[0] = (da * v * sg * (1.0 + u * (1.0 - sg))).astype(BF)
    dv_ref[0] = (da * u * sg).astype(BF)


def dx_kernel(du_ref, dv_ref, w1_ref, w3_ref, o_ref):
    to_sources([dot_nt(du_ref[h], w1_ref[h]) + dot_nt(dv_ref[h], w3_ref[h]) for h in range(2)], o_ref)


def grad_kernel(rank_ref, *refs, el):
    srcs = refs[:ND]
    du_ref, dv_ref, gw1_ref, gw3_ref, xs_ref = refs[ND:]
    e = pl.program_id(0)

    @pl.when(e == 0)
    def _():
        gather_experts(rank_ref, srcs, xs_ref, el)

    xs = xs_ref[e]
    gw1_ref[0] = dot_tn(xs, du_ref[0])
    gw3_ref[0] = dot_tn(xs, dv_ref[0])


def solution(mesh):
    grp = ('row', 'col')
    tspec = P(('dp', 'row', 'col'), None)
    wspec = P(grp, None, None)
    gspec = P(('dp', 'row', 'col'), None, None)

    def permute(a, k):
        return lax.ppermute(a, grp, [(p, p ^ k) for p in range(ND)])

    def gather_tokens(a):
        got = {0: a, 1: permute(a, 1)}
        for k in (2, 4, 6):
            got[k] = permute(a, k)
        for k in (2, 4, 6):
            got[k + 1] = permute(got[k], 1)
        return [got[k] for k in range(ND)]

    def return_sums(send, keep):
        got = permute(send, 1)
        total = keep[0] + got[0]
        for k in range(1, ND // 2):
            total = total + permute(keep[k] + got[k], 2 * k)
        return total.astype(BF)

    def local(x, ridx, gates, w1, w3, w2, dy):
        tok, d = x.shape
        top = ridx.shape[1]
        el, _, ff = w1.shape
        ep = -(-el // 8) * 8
        m = ND * CAP
        rows = el * CAP
        p = (lax.axis_index('row') * mesh.shape['col'] + lax.axis_index('col')).astype(jnp.int32).reshape(1)
        pad = jnp.zeros((8 - top, tok), F32)
        meta = jnp.concatenate([ridx.T.astype(F32), pad, gates.T, pad])
        meta = lax.all_gather(meta, grp)
        xg = gather_tokens(x)
        dyg = gather_tokens(dy)
        smem = pl.BlockSpec(memory_space=pltpu.SMEM)
        sd = jax.ShapeDtypeStruct
        rank, gate = pl.pallas_call(
            functools.partial(route_kernel, el=el, top=top),
            in_specs=[smem, pl.BlockSpec(memory_space=pltpu.VMEM)],
            out_shape=[sd((ND, ep, tok), F32)] * 2,
            name='route')(p, meta)

        tab = whole((ND, ep, tok))
        srcs = [whole((tok, d))] * ND

        def per(shape):
            return pl.BlockSpec((1,) + shape, lambda e: (e,) + (0,) * len(shape))

        def per2(shape):
            return pl.BlockSpec((2,) + shape, lambda e: (e,) + (0,) * len(shape))

        prod = 2.0 * el * m * d * ff
        wb = el * d * ff * 2
        hid = sd((el, m, ff), BF)
        u, v, a = pl.pallas_call(
            functools.partial(up_kernel, el=el), grid=(el,),
            in_specs=[tab] + srcs + [per((d, ff))] * 2,
            out_specs=[per((m, ff))] * 3,
            out_shape=[hid] * 3,
            scratch_shapes=[pltpu.VMEM((el, m, d), BF)],
            compiler_params=params(), cost_estimate=cost(2 * prod, 2 * wb), name='up')(rank, *xg, w1, w3)

        by_src = pl.BlockSpec((ND, 2 * CAP, d), lambda e: (0, e, 0))
        o = pl.pallas_call(
            down_kernel, grid=(el // 2,),
            in_specs=[per2((m, ff)), per2((ff, d))],
            out_specs=by_src,
            out_shape=sd((ND, rows, d), BF),
            compiler_params=params(), cost_estimate=cost(prod, wb), name='down')(a, w2)

        half = ND // 2

        def src_of(i):
            return jnp.where(i < half, 2 * i + 1, 2 * (i - half))

        def src(shape):
            return pl.BlockSpec((1,) + shape, lambda i, *_: (src_of(i),) + (0,) * len(shape))

        send_spec = pl.BlockSpec((1, tok, d), lambda i, *_: (jnp.minimum(i, half - 1), 0, 0))
        keep_spec = pl.BlockSpec((1, tok, d), lambda i, *_: (jnp.maximum(i - half, 0), 0, 0))
        sums = [sd((half, tok, d), F32)] * 2
        ysend, ykeep, dg = pl.pallas_call(
            functools.partial(combine_y_kernel, el=el),
            grid_spec=pltpu.PrefetchScalarGridSpec(
                num_scalar_prefetch=1, grid=(ND,),
                in_specs=[src((ep, tok))] * 2 + [src((rows, d)), src((tok, d))],
                out_specs=[send_spec, keep_spec,
                           pl.BlockSpec((1, ep, tok), lambda i, pr: (pr[0] ^ src_of(i), 0, 0))]),
            out_shape=sums + [sd((ND, ep, tok), F32)],
            compiler_params=params(), cost_estimate=cost(8.0 * ND * rows * tok * d, 2 * ND * rows * d),
            name='combine_y')(p, rank, gate, o, jnp.stack(dyg))

        y = return_sums(ysend, ykeep)

        du, dv, gw2 = pl.pallas_call(
            functools.partial(act_kernel, el=el), grid=(el,),
            in_specs=[tab] * 2 + srcs + [per((ff, d))] + [per((m, ff))] * 3,
            out_specs=[per((m, ff))] * 2 + [per((ff, d))],
            out_shape=[hid] * 2 + [sd((el, ff, d), F32)],
            scratch_shapes=[pltpu.VMEM((el, m, d), BF)],
            compiler_params=params(), cost_estimate=cost(2 * prod, 3 * wb), name='act')(
                rank, gate, *dyg, w2, u, v, a)

        dxo = pl.pallas_call(
            dx_kernel, grid=(el // 2,),
            in_specs=[per2((m, ff))] * 2 + [per2((d, ff))] * 2,
            out_specs=by_src,
            out_shape=sd((ND, rows, d), BF),
            compiler_params=params(), cost_estimate=cost(2 * prod, 2 * wb), name='dx')(du, dv, w1, w3)

        xsend, xkeep = pl.pallas_call(
            functools.partial(combine_dx_kernel, el=el), grid=(ND,),
            in_specs=[src((ep, tok)), src((rows, d))],
            out_specs=[send_spec, keep_spec],
            out_shape=sums,
            compiler_params=params(), cost_estimate=cost(2.0 * ND * rows * tok * d, 2 * ND * rows * d),
            name='combine_dx')(rank, dxo)
        dx = return_sums(xsend, xkeep)

        gw1, gw3 = pl.pallas_call(
            functools.partial(grad_kernel, el=el), grid=(el,),
            in_specs=[tab] + srcs + [per((m, ff))] * 2,
            out_specs=[per((d, ff))] * 2,
            out_shape=[sd((el, d, ff), F32)] * 2,
            scratch_shapes=[pltpu.VMEM((el, m, d), BF)],
            compiler_params=params(), cost_estimate=cost(2 * prod, 4 * wb), name='grad')(rank, *xg, du, dv)

        dgall = lax.all_to_all(dg, grp, 0, 0, tiled=True)[:, :el].reshape(ND * el, tok).T
        pick = ridx[:, :, None] == jnp.arange(ND * el, dtype=jnp.int32)
        dgates = jnp.sum(jnp.where(pick, dgall[:, None, :], 0.0), axis=2)
        return y, dx, dgates, gw1, gw3, gw2

    return jax.shard_map(local, mesh=mesh, in_specs=(tspec, tspec, tspec, wspec, wspec, wspec, tspec),
                         out_specs=(tspec, tspec, tspec, gspec, gspec, gspec), check_vma=False)
```

time: 583 us -> 291 us (0.50)
  local copies, waits for them, and re-layouts: 223 us -> 3.5 us
  Pallas kernels: 0 us -> 165 us
  matrix products: 157 us -> 0 us
  waiting for transfers between devices: 165 us -> 63.3 us
  blocking collectives: 0 us -> 23.7 us
    all_to_all x4 -> x1, waiting for transfers between devices: 165 us -> 0.01 us  [local(): lax.all_to_all(dg, grp, 0, 0, tiled=True)[:, :el].reshape(ND * el, tok)]
    pallas_call x0 -> x8, Pallas kernels: none -> 165 us  [the longest x1 37.2 us: local(): pl.pallas_call(functools.partial(act_kernel, el=el), grid=(el,), in_specs...]
    dot_general x10 -> x0, matrix products: 157 us -> none  [the longest x1 23 us: expert_backward(): gw2 = jnp.einsum('ecf,ecd->efd', a, doe, preferred_element_type=jnp.float32)]
    gather x15 -> x0, local copies, waits for them, and re-layouts: 77.1 us -> none  [the longest x10 31.9 us: slot_positions(): first = jnp.searchsorted(es, es, side='left').astype(jnp.int32)]
    reshape x9 -> x1, local copies, waits for them, and re-layouts: 72.3 us -> 0.01 us  [local(): lax.all_to_all(dg, grp, 0, 0, tiled=True)[:, :el].reshape(ND * el, tok)]
    ppermute x0 -> x22, waiting for transfers between devices: none -> 63.3 us  [permute(): return lax.ppermute(a, grp, [(p, p ^ k) for p in range(ND)])]
    transpose x4 -> x0, local copies, waits for them, and re-layouts: 37.6 us -> none  [the longest x2 19.1 us: to_experts(): buf.reshape(nd, el, cap, d).transpose(1, 0, 2, 3).reshape(el, nd * cap, d)]
    all_gather x0 -> x1, blocking collectives: none -> 23.7 us  [local(): meta = lax.all_gather(meta, grp)]
  transfers between devices with their start and end apart: 4 -> 23, of which waited for: 4 -> 7; matrix products, arithmetic and copies ran while one was open for 35% -> 4% of each run, Pallas kernels for 0% -> 52%
where the time goes in v1:
time: 291 us; the launch traced here: 289 us
  Pallas kernels  165 us (57%)
  waiting for transfers between devices  63.3 us (22%)
  blocking collectives  23.7 us (8%)
  starting transfers between devices  21.2 us (7%)
  other arithmetic  11.4 us (4%)
  local copies, waits for them, and re-layouts  3.5 us (1%)
    ppermute x22, waiting for transfers between devices, permute(): return lax.ppermute(a, grp, [(p, p ^ k) for p in range(ND)])  63.3 us
    pallas_call x1, Pallas kernels, local(): pl.pallas_call(functools.partial(act_kernel, el=el), grid=(el,), in_specs...  37.2 us
    pallas_call x1, Pallas kernels, local(): pl.pallas_call(functools.partial(grad_kernel, el=el), grid=(el,), in_spec...  32.1 us
    pallas_call x1, Pallas kernels, local(): pl.pallas_call(functools.partial(up_kernel, el=el), grid=(el,), in_specs=...  29.2 us
    pallas_call x1, Pallas kernels, local(): pl.pallas_call(dx_kernel, grid=(el // 2,), in_specs=[per2((m, ff))] * 2 +...  24.6 us
    all_gather x1, blocking collectives, local(): meta = lax.all_gather(meta, grp)  23.7 us
    ppermute x22, starting transfers between devices, permute(): return lax.ppermute(a, grp, [(p, p ^ k) for p in range(ND)])  18.9 us
    pallas_call x1, Pallas kernels, local(): pl.pallas_call(down_kernel, grid=(el // 2,), in_specs=[per2((m, ff)), per...  16.2 us
  transfers between devices with their start and end apart: 23, of which 7 were waited for; matrix products, arithmetic and copies ran while one was open for 4% of the time, Pallas kernels for 52%

profile of v1, /device:TPU:0, one launch (start us, length us, event | category | flops | bytes accessed | tf_op | source)
XLA Modules:
  0.0 288.9 jit_solution(11644366229346761924)
XLA Ops:
  0.6 4.3 %collective-permute-start.5 = (bf16[128,1280]{1,0:T(8,128)(2,1)}, bf16[128,1280]{1,0:T(8,128)(2,1)S(1)}, u32[]{:S(2)}, u32[]{:S(2)}) collective-permute-start(bf16[128,1280]{1,0:T(8,128)(2,1)} %refs_0_.5), channel_id=1, source_target_pairs={{0,6},{1,7},{2,4},{3,5},{4,2},{5,3},{6,0},{7,1}} | collective-permute-start | bytes 983048 | tf_op jit(solution)/shard_map/ppermute | solution.py:207
  5.0 0.5 collective-permute-start.3
  5.5 0.1 collective-permute-start.1
  5.6 1.9 collective-permute-start.8
  7.5 0.7 convert_bitcast_fusion
  8.2 0.7 pad_maximum_fusion
  8.9 23.7 %all-gather = f32[128,128]{1,0:T(8,128)} all-gather(f32[16,128]{1,0:T(8,128)S(1)} %pad_maximum_fusion), channel_id=2, replica_groups=mesh['dp'=1,'row'=2,'col'=4] {'row','col'}, dimensions={0}, use_global_device_ids=true | all-gather | bytes 73728 | tf_op jit(solution)/shard_map/all_gather | solution.py:234
  32.6 1.7 route.1
  34.3 1.0 bitcast_dynamic-update-slice_fusion.7
  35.3 1.5 collective-permute-start.10
  36.9 6.9 %collective-permute-done.10.refs_4_ = bf16[128,1280]{1,0:T(8,128)(2,1)S(1)} collective-permute-done((bf16[128,1280]{1,0:T(8,128)(2,1)}, bf16[128,1280]{1,0:T(8,128)(2,1)S(1)}, u32[]{:S(2)}, u32[]{:S(2)}) %collective-permute-start.10) | collective-permute-done | bytes 327712 | tf_op jit(solution)/shard_map/ppermute | solution.py:207
  43.9 1.5 collective-permute-start.12
  45.4 0.5 collective-permute-start
  46.0 0.0 collective-permute-start.6
  46.0 0.5 collective-permute-start.4
  46.5 6.3 %collective-permute-done.12.refs_6_ = bf16[128,1280]{1,0:T(8,128)(2,1)S(1)} collective-permute-done((bf16[128,1280]{1,0:T(8,128)(2,1)}, bf16[128,1280]{1,0:T(8,128)(2,1)S(1)}, u32[]{:S(2)}, u32[]{:S(2)}) %collective-permute-start.12) | collective-permute-done | bytes 327712 | tf_op jit(solution)/shard_map/ppermute | solution.py:207
  52.8 0.5 collective-permute-start.13
  53.5 1.0 collective-permute-done.2.refs_3_
  54.4 0.4 copy-done.16
  54.9 0.1 copy-done.12
  55.0 0.1 copy-done.13
  55.1 0.1 copy-done.14
  55.2 0.7 copy-done.15
  55.9 29.2 %up.1 = (bf16[20,192,384]{2,1,0:T(8,128)(2,1)}, bf16[20,192,384]{2,1,0:T(8,128)(2,1)}, bf16[20,192,384]{2,1,0:T(8,128)(2,1)}) custom-call(f32[8,24,128]{2,1,0:T(8,128)} %get-tuple-element.21.rank_ref, bf16[128,1280]{1,0:T(8,128)(2,1)} %refs_0_.5, bf16[128,1280]{1,0:T(8,128)(2,1)} %copy-done.12, bf16[128,1280]{1,0:T(8,128)(2,1)} %copy-done.11, ...), custom_call_target="tpu_custom_call" | custom-call | flops 7549747200 | bytes 39321600 | tf_op jit(solution)/shard_map/up/pallas_call | solution.py:257
  85.2 16.2 %down.1.o_ref = bf16[8,480,1280]{2,1,0:T(8,128)(2,1)} custom-call(bf16[20,192,384]{2,1,0:T(8,128)(2,1)} %get-tuple-element.23.a_ref.refs_11_, bf16[20,384,1280]{2,1,0:T(8,128)(2,1)} %refs_8_.3), custom_call_target="tpu_custom_call" | custom-call | flops 3774873600 | bytes 19660800 | tf_op jit(solution)/shard_map/down/pallas_call | solution.py:266
  101.4 0.8 bitcast_dynamic-update-slice_fusion.dy_ref
  102.2 13.8 %combine_y.1 = (f32[4,128,1280]{2,1,0:T(8,128)}, f32[4,128,1280]{2,1,0:T(8,128)}, f32[8,24,128]{2,1,0:T(8,128)}) custom-call(s32[1]{0:T(128)} %bitcast.p_ref, f32[8,24,128]{2,1,0:T(8,128)} %get-tuple-element.21.rank_ref, f32[8,24,128]{2,1,0:T(8,128)} %get-tuple-element.22.gate_ref, bf16[8,480,1280]{2,1,0:T(8,128)(2,1)} %down.1.o_ref, ...), custom_call_target="tpu_custom_call" | custom-call | flops 5033164800 | bytes 9830400 | tf_op jit(solution)/shard_map/combine_y/pallas_call | solution.py:284
  116.0 37.2 %act.1 = (bf16[20,192,384]{2,1,0:T(8,128)(2,1)}, bf16[20,192,384]{2,1,0:T(8,128)(2,1)}, f32[20,384,1280]{2,1,0:T(8,128)}) custom-call(f32[8,24,128]{2,1,0:T(8,128)} %get-tuple-element.21.rank_ref, f32[8,24,128]{2,1,0:T(8,128)} %get-tuple-element.22.gate_ref, bf16[128,1280]{1,0:T(8,128)(2,1)} %refs_0_.4, bf16[128,1280]{1,0:T(8,128)(2,1)} %copy-done.2, ...), custom_call_target="tpu_custom_call" | custom-call | flops 7549747200 | bytes 58982400 | tf_op jit(solution)/shard_map/act/pallas_call | solution.py:297
  153.3 24.6 %dx.1.o_ref = bf16[8,480,1280]{2,1,0:T(8,128)(2,1)} custom-call(bf16[20,192,384]{2,1,0:T(8,128)(2,1)} %get-tuple-element.28.du_ref.refs_8_, bf16[20,192,384]{2,1,0:T(8,128)(2,1)} %get-tuple-element.29.dv_ref.refs_9_, bf16[20,1280,384]{2,1,0:T(8,128)(2,1)} %w1_ref.1, bf16[20,1280,384]{2,1,0:T(8,128)(2,1)} %w3_ref.1), custom_call_target="tpu_custom_call" | custom-call | flops 7549747200 | bytes 39321600 | tf_op jit(solution)/shard_map/dx/pallas_call | solution.py:306
  177.9 10.0 %combine_dx.1 = (f32[4,128,1280]{2,1,0:T(8,128)}, f32[4,128,1280]{2,1,0:T(8,128)}) custom-call(f32[8,24,128]{2,1,0:T(8,128)} %get-tuple-element.21.rank_ref, bf16[8,480,1280]{2,1,0:T(8,128)(2,1)} %dx.1.o_ref), custom_call_target="tpu_custom_call" | custom-call | flops 1258291200 | bytes 9830400 | tf_op jit(solution)/shard_map/combine_dx/pallas_call | solution.py:313
  187.9 0.5 collective-permute-start.18
  188.3 2.3 all-to-all-start
  190.6 2.8 fusion.10
  193.5 1.7 collective-permute-start.15
  195.2 32.1 %grad.1 = (f32[20,1280,384]{2,1,0:T(8,128)}, f32[20,1280,384]{2,1,0:T(8,128)}) custom-call(f32[8,24,128]{2,1,0:T(8,128)} %get-tuple-element.21.rank_ref, bf16[128,1280]{1,0:T(8,128)(2,1)} %refs_0_.5, bf16[128,1280]{1,0:T(8,128)(2,1)} %copy-done.12, bf16[128,1280]{1,0:T(8,128)(2,1)} %copy-done.11, bf16[128,1280]{1,0:T(8,128)(2,1)} %copy-done.15, ...), custom_call_target="tpu_custom_call" | custom-call | flops 7549747200 | bytes 78643200 | tf_op jit(solution)/shard_map/grad/pallas_call | solution.py:322
  227.3 1.5 collective-permute-start.17
  228.8 0.3 collective-permute-start.16
  229.1 2.3 fusion.2
  231.4 1.8 collective-permute-start.19
  233.2 1.5 collective-permute-start.21
  234.7 0.3 collective-permute-start.20
  234.9 0.7 select_reduce_fusion
  235.6 10.3 %collective-permute-done.17 = f32[128,1280]{1,0:T(8,128)S(1)} collective-permute-done((f32[128,1280]{1,0:T(8,128)}, f32[128,1280]{1,0:T(8,128)S(1)}, u32[]{:S(2)}, u32[]{:S(2)}) %collective-permute-start.17) | collective-permute-done | bytes 655392 | tf_op jit(solution)/shard_map/ppermute | solution.py:207
  246.0 14.0 %collective-permute-done.16 = f32[128,1280]{1,0:T(8,128)S(1)} collective-permute-done((f32[128,1280]{1,0:T(8,128)}, f32[128,1280]{1,0:T(8,128)S(1)}, u32[]{:S(2)}, u32[]{:S(2)}) %collective-permute-start.16) | collective-permute-done | bytes 655392 | tf_op jit(solution)/shard_map/ppermute | solution.py:207
  259.9 2.0 fusion.15
  262.0 11.2 %collective-permute-done.21 = f32[128,1280]{1,0:T(8,128)S(1)} collective-permute-done((f32[128,1280]{1,0:T(8,128)S(1)}, f32[128,1280]{1,0:T(8,128)S(1)}, u32[]{:S(2)}, u32[]{:S(2)}) %collective-permute-start.21) | collective-permute-done | bytes 655392 | tf_op jit(solution)/shard_map/ppermute | solution.py:207
  273.1 13.5 %collective-permute-done.20 = f32[128,1280]{1,0:T(8,128)S(1)} collective-permute-done((f32[128,1280]{1,0:T(8,128)S(1)}, f32[128,1280]{1,0:T(8,128)S(1)}, u32[]{:S(2)}, u32[]{:S(2)}) %collective-permute-start.20) | collective-permute-done | bytes 655392 | tf_op jit(solution)/shard_map/ppermute | solution.py:207
  286.7 2.2 fusion.7
  (60 shorter events, 0.3 us)
Async XLA Ops:
  0.6 44.8 %copy-start.8 = (bf16[128,1280]{1,0:T(8,128)(2,1)S(1)}, bf16[128,1280]{1,0:T(8,128)(2,1)}, u32[]{:S(2)}) copy-start(bf16[128,1280]{1,0:T(8,128)(2,1)} %refs_0_.5) | copy-start | bytes 983044
  0.6 44.8 %collective-permute-start.5 = (bf16[128,1280]{1,0:T(8,128)(2,1)}, bf16[128,1280]{1,0:T(8,128)(2,1)S(1)}, u32[]{:S(2)}, u32[]{:S(2)}) collective-permute-start(bf16[128,1280]{1,0:T(8,128)(2,1)} %refs_0_.5), channel_id=1, source_target_pairs={{0,6},{1,7},{2,4},{3,5},{4,2},{5,3},{6,0},{7,1}} | collective-permute-start | bytes 983048 | tf_op jit(solution)/shard_map/ppermute | solution.py:207
  5.0 41.0 %collective-permute-start.3 = (bf16[128,1280]{1,0:T(8,128)(2,1)}, bf16[128,1280]{1,0:T(8,128)(2,1)S(1)}, u32[]{:S(2)}, u32[]{:S(2)}) collective-permute-start(bf16[128,1280]{1,0:T(8,128)(2,1)} %refs_0_.5), channel_id=1, source_target_pairs={{0,4},{1,5},{2,6},{3,7},{4,0},{5,1},{6,2},{7,3}} | collective-permute-start | bytes 983048 | tf_op jit(solution)/shard_map/ppermute | solution.py:207
  5.5 40.6 %collective-permute-start.1 = (bf16[128,1280]{1,0:T(8,128)(2,1)}, bf16[128,1280]{1,0:T(8,128)(2,1)S(1)}, u32[]{:S(2)}, u32[]{:S(2)}) collective-permute-start(bf16[128,1280]{1,0:T(8,128)(2,1)} %refs_0_.5), channel_id=1, source_target_pairs={{0,2},{1,3},{2,0},{3,1},{4,6},{5,7},{6,4},{7,5}} | collective-permute-start | bytes 983048 | tf_op jit(solution)/shard_map/ppermute | solution.py:207
  5.6 29.8 %collective-permute-start.8 = (bf16[128,1280]{1,0:T(8,128)(2,1)}, bf16[128,1280]{1,0:T(8,128)(2,1)S(1)}, u32[]{:S(2)}, u32[]{:S(2)}) collective-permute-start(bf16[128,1280]{1,0:T(8,128)(2,1)} %refs_0_.4), channel_id=1, source_target_pairs={{0,2},{1,3},{2,0},{3,1},{4,6},{5,7},{6,4},{7,5}} | collective-permute-start | bytes 983048 | tf_op jit(solution)/shard_map/ppermute | solution.py:207
  7.5 29.4 %collective-permute-start.7 = (bf16[128,1280]{1,0:T(8,128)(2,1)}, bf16[128,1280]{1,0:T(8,128)(2,1)S(1)}, u32[]{:S(2)}, u32[]{:S(2)}) collective-permute-start(bf16[128,1280]{1,0:T(8,128)(2,1)} %refs_0_.4), channel_id=1, source_target_pairs={{0,1},{1,0},{2,3},{3,2},{4,5},{5,4},{6,7},{7,6}} | collective-permute-start | bytes 983048 | tf_op jit(solution)/shard_map/ppermute | solution.py:207
  35.3 49.8 %copy-start.1 = (bf16[128,1280]{1,0:T(8,128)(2,1)}, bf16[128,1280]{1,0:T(8,128)(2,1)S(1)}, u32[]{:S(2)}) copy-start(bf16[128,1280]{1,0:T(8,128)(2,1)S(1)} %collective-permute-done.8.refs_2_) | copy-start | bytes 983044
  35.3 8.5 %collective-permute-start.10 = (bf16[128,1280]{1,0:T(8,128)(2,1)}, bf16[128,1280]{1,0:T(8,128)(2,1)S(1)}, u32[]{:S(2)}, u32[]{:S(2)}) collective-permute-start(bf16[128,1280]{1,0:T(8,128)(2,1)} %refs_0_.4), channel_id=1, source_target_pairs={{0,4},{1,5},{2,6},{3,7},{4,0},{5,1},{6,2},{7,3}} | collective-permute-start | bytes 983048 | tf_op jit(solution)/shard_map/ppermute | solution.py:207
  36.9 48.3 %copy-start.2 = (bf16[128,1280]{1,0:T(8,128)(2,1)}, bf16[128,1280]{1,0:T(8,128)(2,1)S(1)}, u32[]{:S(2)}) copy-start(bf16[128,1280]{1,0:T(8,128)(2,1)S(1)} %collective-permute-done.7.refs_1_) | copy-start | bytes 983044
  36.9 8.5 %collective-permute-start.9 = (bf16[128,1280]{1,0:T(8,128)(2,1)S(1)}, bf16[128,1280]{1,0:T(8,128)(2,1)S(1)}, u32[]{:S(2)}, u32[]{:S(2)}) collective-permute-start(bf16[128,1280]{1,0:T(8,128)(2,1)S(1)} %collective-permute-done.8.refs_2_), channel_id=1, source_target_pairs={{0,1},{1,0},{2,3},{3,2},{4,5},{5,4},{6,7},{7,6}} | collective-permute-start | bytes 983048 | tf_op jit(solution)/shard_map/ppermute | solution.py:207
  43.9 41.3 %copy-start.3 = (bf16[128,1280]{1,0:T(8,128)(2,1)}, bf16[128,1280]{1,0:T(8,128)(2,1)S(1)}, u32[]{:S(2)}) copy-start(bf16[128,1280]{1,0:T(8,128)(2,1)S(1)} %collective-permute-done.10.refs_4_) | copy-start | bytes 983044
  43.9 8.9 %collective-permute-start.12 = (bf16[128,1280]{1,0:T(8,128)(2,1)}, bf16[128,1280]{1,0:T(8,128)(2,1)S(1)}, u32[]{:S(2)}, u32[]{:S(2)}) collective-permute-start(bf16[128,1280]{1,0:T(8,128)(2,1)} %refs_0_.4), channel_id=1, source_target_pairs={{0,6},{1,7},{2,4},{3,5},{4,2},{5,3},{6,0},{7,1}} | collective-permute-start | bytes 983048 | tf_op jit(solution)/shard_map/ppermute | solution.py:207
  45.3 39.8 %copy-start.4 = (bf16[128,1280]{1,0:T(8,128)(2,1)}, bf16[128,1280]{1,0:T(8,128)(2,1)S(1)}, u32[]{:S(2)}) copy-start(bf16[128,1280]{1,0:T(8,128)(2,1)S(1)} %collective-permute-done.9.refs_3_) | copy-start | bytes 983044
  45.3 7.5 %collective-permute-start.11 = (bf16[128,1280]{1,0:T(8,128)(2,1)S(1)}, bf16[128,1280]{1,0:T(8,128)(2,1)S(1)}, u32[]{:S(2)}, u32[]{:S(2)}) collective-permute-start(bf16[128,1280]{1,0:T(8,128)(2,1)S(1)} %collective-permute-done.10.refs_4_), channel_id=1, source_target_pairs={{0,1},{1,0},{2,3},{3,2},{4,5},{5,4},{6,7},{7,6}} | collective-permute-start | bytes 983048 | tf_op jit(solution)/shard_map/ppermute | solution.py:207
  45.4 10.5 %copy-start.9 = (bf16[128,1280]{1,0:T(8,128)(2,1)}, bf16[128,1280]{1,0:T(8,128)(2,1)S(1)}, u32[]{:S(2)}) copy-start(bf16[128,1280]{1,0:T(8,128)(2,1)S(1)} %collective-permute-done.5.refs_6_) | copy-start | bytes 983044
  45.4 8.0 %collective-permute-start = (bf16[128,1280]{1,0:T(8,128)(2,1)S(1)}, bf16[128,1280]{1,0:T(8,128)(2,1)S(1)}, u32[]{:S(2)}, u32[]{:S(2)}) collective-permute-start(bf16[128,1280]{1,0:T(8,128)(2,1)S(1)} %copy-done.8), channel_id=1, source_target_pairs={{0,1},{1,0},{2,3},{3,2},{4,5},{5,4},{6,7},{7,6}} | collective-permute-start | bytes 983048 | tf_op jit(solution)/shard_map/ppermute | solution.py:207
  46.0 10.0 %copy-start.10 = (bf16[128,1280]{1,0:T(8,128)(2,1)}, bf16[128,1280]{1,0:T(8,128)(2,1)S(1)}, u32[]{:S(2)}) copy-start(bf16[128,1280]{1,0:T(8,128)(2,1)S(1)} %collective-permute-done.3.refs_4_) | copy-start | bytes 983044
  46.0 7.5 %collective-permute-start.6 = (bf16[128,1280]{1,0:T(8,128)(2,1)S(1)}, bf16[128,1280]{1,0:T(8,128)(2,1)S(1)}, u32[]{:S(2)}, u32[]{:S(2)}) collective-permute-start(bf16[128,1280]{1,0:T(8,128)(2,1)S(1)} %collective-permute-done.5.refs_6_), channel_id=1, source_target_pairs={{0,1},{1,0},{2,3},{3,2},{4,5},{5,4},{6,7},{7,6}} | collective-permute-start | bytes 983048 | tf_op jit(solution)/shard_map/ppermute | solution.py:207
  46.0 9.9 %copy-start.11 = (bf16[128,1280]{1,0:T(8,128)(2,1)}, bf16[128,1280]{1,0:T(8,128)(2,1)S(1)}, u32[]{:S(2)}) copy-start(bf16[128,1280]{1,0:T(8,128)(2,1)S(1)} %collective-permute-done.1.refs_2_) | copy-start | bytes 983044
  46.0 7.4 %collective-permute-start.4 = (bf16[128,1280]{1,0:T(8,128)(2,1)S(1)}, bf16[128,1280]{1,0:T(8,128)(2,1)S(1)}, u32[]{:S(2)}, u32[]{:S(2)}) collective-permute-start(bf16[128,1280]{1,0:T(8,128)(2,1)S(1)} %collective-permute-done.3.refs_4_), channel_id=1, source_target_pairs={{0,1},{1,0},{2,3},{3,2},{4,5},{5,4},{6,7},{7,6}} | collective-permute-start | bytes 983048 | tf_op jit(solution)/shard_map/ppermute | solution.py:207
  52.8 32.4 %copy-start.5 = (bf16[128,1280]{1,0:T(8,128)(2,1)}, bf16[128,1280]{1,0:T(8,128)(2,1)S(1)}, u32[]{:S(2)}) copy-start(bf16[128,1280]{1,0:T(8,128)(2,1)S(1)} %collective-permute-done.12.refs_6_) | copy-start | bytes 983044
  52.8 1.6 collective-permute-start.2
  52.8 32.4 %copy-start.6 = (bf16[128,1280]{1,0:T(8,128)(2,1)}, bf16[128,1280]{1,0:T(8,128)(2,1)S(1)}, u32[]{:S(2)}) copy-start(bf16[128,1280]{1,0:T(8,128)(2,1)S(1)} %collective-permute-done.11.refs_5_) | copy-start | bytes 983044
  52.8 48.5 %collective-permute-start.13 = (bf16[128,1280]{1,0:T(8,128)(2,1)S(1)}, bf16[128,1280]{1,0:T(8,128)(2,1)S(1)}, u32[]{:S(2)}, u32[]{:S(2)}) collective-permute-start(bf16[128,1280]{1,0:T(8,128)(2,1)S(1)} %collective-permute-done.12.refs_6_), channel_id=1, source_target_pairs={{0,1},{1,0},{2,3},{3,2},{4,5},{5,4},{6,7},{7,6}} | collective-permute-start | bytes 983048 | tf_op jit(solution)/shard_map/ppermute | solution.py:207
  53.4 1.5 copy-start.16
  53.4 1.6 copy-start.12
  53.4 1.6 copy-start.13
  53.5 1.7 copy-start.14
  55.2 0.7 copy-start.15
  101.4 14.6 %copy-start.7 = (bf16[128,1280]{1,0:T(8,128)(2,1)}, bf16[128,1280]{1,0:T(8,128)(2,1)S(1)}, u32[]{:S(2)}) copy-start(bf16[128,1280]{1,0:T(8,128)(2,1)S(1)} %collective-permute-done.13.refs_7_) | copy-start | bytes 983044
  116.0 74.6 %collective-permute-start.14 = (f32[4,128,1280]{2,1,0:T(8,128)}, f32[4,128,1280]{2,1,0:T(8,128)}, u32[]{:S(2)}, u32[]{:S(2)}) collective-permute-start(f32[4,128,1280]{2,1,0:T(8,128)} %get-tuple-element.25), channel_id=1, source_target_pairs={{0,1},{1,0},{2,3},{3,2},{4,5},{5,4},{6,7},{7,6}} | collective-permute-start | bytes 7864328 | tf_op jit(solution)/shard_map/ppermute | solution.py:207
  177.9 12.8 %copy-start = (f32[4,128,1280]{2,1,0:T(8,128)S(1)}, f32[4,128,1280]{2,1,0:T(8,128)}, u32[]{:S(2)}) copy-start(f32[4,128,1280]{2,1,0:T(8,128)} %get-tuple-element.24) | copy-start | bytes 7864324
  187.9 41.3 %collective-permute-start.18 = (f32[4,128,1280]{2,1,0:T(8,128)}, f32[4,128,1280]{2,1,0:T(8,128)}, u32[]{:S(2)}, u32[]{:S(2)}) collective-permute-start(f32[4,128,1280]{2,1,0:T(8,128)} %get-tuple-element.31), channel_id=1, source_target_pairs={{0,1},{1,0},{2,3},{3,2},{4,5},{5,4},{6,7},{7,6}} | collective-permute-start | bytes 7864328 | tf_op jit(solution)/shard_map/ppermute | solution.py:207
  188.3 39.0 %all-to-all-start = ((f32[8,24,128]{2,1,0:T(8,128)}), f32[8,24,128]{2,1,0:T(8,128)S(1)}, u32[]{:S(2)}, u32[]{:S(2)}) async-start(f32[8,24,128]{2,1,0:T(8,128)} %get-tuple-element.32), calls=%async_computation | async-start | bytes 196608 | tf_op jit(solution)/shard_map/all_to_all | solution.py:330
  193.5 41.2 %collective-permute-start.15 = (f32[128,1280]{1,0:T(8,128)}, f32[128,1280]{1,0:T(8,128)S(1)}, u32[]{:S(2)}, u32[]{:S(2)}) collective-permute-start(f32[128,1280]{1,0:T(8,128)} %get-tuple-element.39), channel_id=1, source_target_pairs={{0,2},{1,3},{2,0},{3,1},{4,6},{5,7},{6,4},{7,5}} | collective-permute-start | bytes 1966088 | tf_op jit(solution)/shard_map/ppermute | solution.py:207
  227.3 18.6 %collective-permute-start.17 = (f32[128,1280]{1,0:T(8,128)}, f32[128,1280]{1,0:T(8,128)S(1)}, u32[]{:S(2)}, u32[]{:S(2)}) collective-permute-start(f32[128,1280]{1,0:T(8,128)} %get-tuple-element.40), channel_id=1, source_target_pairs={{0,6},{1,7},{2,4},{3,5},{4,2},{5,3},{6,0},{7,1}} | collective-permute-start | bytes 1966088 | tf_op jit(solution)/shard_map/ppermute | solution.py:207
  228.8 31.1 %collective-permute-start.16 = (f32[128,1280]{1,0:T(8,128)}, f32[128,1280]{1,0:T(8,128)S(1)}, u32[]{:S(2)}, u32[]{:S(2)}) collective-permute-start(f32[128,1280]{1,0:T(8,128)} %get-tuple-element.41), channel_id=1, source_target_pairs={{0,4},{1,5},{2,6},{3,7},{4,0},{5,1},{6,2},{7,3}} | collective-permute-start | bytes 1966088 | tf_op jit(solution)/shard_map/ppermute | solution.py:207
  229.1 5.8 %copy-start.17 = (s32[128,6]{0,1:T(8,128)S(1)}, s32[128,6]{0,1:T(8,128)}, u32[]{:S(2)}) copy-start(s32[128,6]{0,1:T(8,128)} %param.8) | copy-start | bytes 9220
  231.4 30.5 %collective-permute-start.19 = (f32[128,1280]{1,0:T(8,128)S(1)}, f32[128,1280]{1,0:T(8,128)S(1)}, u32[]{:S(2)}, u32[]{:S(2)}) collective-permute-start(f32[128,1280]{1,0:T(8,128)S(1)} %get-tuple-element.36), channel_id=1, source_target_pairs={{0,2},{1,3},{2,0},{3,1},{4,6},{5,7},{6,4},{7,5}} | collective-permute-start | bytes 1966088 | tf_op jit(solution)/shard_map/ppermute | solution.py:207
  233.2 40.0 %collective-permute-start.21 = (f32[128,1280]{1,0:T(8,128)S(1)}, f32[128,1280]{1,0:T(8,128)S(1)}, u32[]{:S(2)}, u32[]{:S(2)}) collective-permute-start(f32[128,1280]{1,0:T(8,128)S(1)} %get-tuple-element.37), channel_id=1, source_target_pairs={{0,6},{1,7},{2,4},{3,5},{4,2},{5,3},{6,0},{7,1}} | collective-permute-start | bytes 1966088 | tf_op jit(solution)/shard_map/ppermute | solution.py:207
  234.7 52.0 %collective-permute-start.20 = (f32[128,1280]{1,0:T(8,128)S(1)}, f32[128,1280]{1,0:T(8,128)S(1)}, u32[]{:S(2)}, u32[]{:S(2)}) collective-permute-start(f32[128,1280]{1,0:T(8,128)S(1)} %get-tuple-element.38), channel_id=1, source_target_pairs={{0,4},{1,5},{2,6},{3,7},{4,0},{5,1},{6,2},{7,3}} | collective-permute-start | bytes 1966088 | tf_op jit(solution)/shard_map/ppermute | solution.py:207
